TPU v7x, 32 devices: a whole 2x2x4 slice. The times are simulated.
32 devices in a mesh: row: 8 (over y, x, core), col: 4 (over z).
Axes of the slice: x: 2, y: 2, z: 4, core: 2. Of those that a mesh axis runs over, the one named last changes fastest.
Arguments:
- src_points: bfloat16 [8192, 256], P('row'), may hold values from -32 to 32, as said below
- tgt_points: bfloat16 [16384, 256], P(('col', 'row')), may hold values from -32 to 32, as said below
- log_src_mass: float32 [8192], P('row'), may hold values from -3 to 3
- log_tgt_mass: float32 [16384], P('col'), may hold values from -3 to 3
Outputs:
- src_potential: float32 [8192], P('row')
- tgt_potential: float32 [16384], P('col')
- mean_potentials: float32 [], replicated
Inputs may be any that keep to these rules, and one draw needn't show every extreme that they name: `src_points`: point coordinates. `tgt_points`: point coordinates.
All inputs are finite; a program needn't handle non-finite values.
Results may differ from a plain program's by a relative error of at most 0.0003.
Values may be sent and summed in bfloat16 or wider, within the bound.
A program may use at most 64 MiB of HBM per device.

v0:
```python
import jax
import jax.numpy as jnp
from jax import lax
from jax.sharding import PartitionSpec as P

ITERS = 3
entropy_weight = 0.1


def combined_all(value, axis, combine):
    everything = jax.tree.map(lambda part: lax.all_gather(part, axis), value)
    leading = jax.tree.map(lambda part: part[0], everything)

    def turn(k, so_far):
        return combine(so_far, jax.tree.map(lambda part: part[k], everything))

    return lax.fori_loop(1, lax.axis_size(axis), turn, leading)


def cost_block(points_a, squares_a, points_b, squares_b):
    product = lax.dot_general(
        points_a, points_b, (((1,), (1,)), ((), ())), preferred_element_type=jnp.float32
    )
    return (squares_a[:, None] + squares_b[None, :] - 2.0 * product) / points_a.shape[1]


def combine(early, later):
    top = jnp.maximum(early[0], later[0])
    return (top, early[1] * jnp.exp(early[0] - top) + later[1] * jnp.exp(later[0] - top))


def body(src_points, tgt_points, log_src_mass, log_tgt_mass):
    targets = lax.all_gather(tgt_points, "row", axis=0, tiled=True)
    sqy = jnp.sum(targets.astype(jnp.float32) ** 2, axis=1)
    count = src_points.shape[0]
    block = min(256, count)
    blocks = count // block
    src_blocks = src_points.reshape(blocks, block, -1)
    sq_blocks = jnp.sum(src_points.astype(jnp.float32) ** 2, axis=1).reshape(blocks, block)
    mass_blocks = log_src_mass.reshape(blocks, block)
    width_tgt = targets.shape[0]
    tgt_potential = jnp.zeros((width_tgt,), jnp.float32)
    src_potential = jnp.zeros((count,), jnp.float32)
    for step in range(ITERS):

        def row_terms(points, squares):
            cost = cost_block(points, squares, targets, sqy)
            return log_tgt_mass[None, :] + (tgt_potential[None, :] - cost) / entropy_weight

        def row_pair(item):
            terms = row_terms(item[0], item[1])
            top = jnp.max(terms, axis=1)
            return (top, jnp.sum(jnp.exp(terms - top[:, None]), axis=1))

        top, total = lax.map(row_pair, (src_blocks, sq_blocks))
        top, total = combined_all((top.reshape(-1), total.reshape(-1)), "col", combine)
        src_potential = -entropy_weight * (top + jnp.log(total))
        pot_blocks = src_potential.reshape(blocks, block)

        def col_terms(points, squares, mass, pot):
            cost = cost_block(points, squares, targets, sqy)
            return mass[:, None] + (pot[:, None] - cost) / entropy_weight

        def pair_step(carry, item):
            terms = col_terms(item[0], item[1], item[2], item[3])
            block_top = jnp.max(terms, axis=0)
            block_sum = jnp.sum(jnp.exp(terms - block_top[None, :]), axis=0)
            return (combine(carry, (block_top, block_sum)), None)

        start = (
            jnp.full((width_tgt,), -jnp.inf, jnp.float32),
            jnp.zeros((width_tgt,), jnp.float32),
        )
        inputs = (src_blocks, sq_blocks, mass_blocks, pot_blocks)
        (top, total), unused = lax.scan(pair_step, start, inputs)
        top, total = combined_all((top, total), "row", combine)
        tgt_potential = -entropy_weight * (top + jnp.log(total))
    sources_all = count * lax.axis_size("row")
    targets_all = width_tgt * lax.axis_size("col")
    local = jnp.sum(src_potential) / (sources_all * lax.axis_size("col")) + jnp.sum(
        tgt_potential
    ) / (targets_all * lax.axis_size("row"))
    mean_potentials = lax.psum(local, ("row", "col"))
    return (src_potential, tgt_potential, mean_potentials)


def solution(mesh):
    return jax.shard_map(
        body,
        mesh=mesh,
        in_specs=(P("row", None), P(("col", "row"), None), P("row"), P("col")),
        out_specs=(P("row"), P("col"), P()),
        check_vma=False,
    )
```

profile of v0, /device:TPU:0, one launch (start us, length us, event | category | flops | bytes accessed | tf_op | source)
XLA Modules:
  0.0 320.3 jit_solution(3803695196308315043)
XLA Ops:
  9.9 30.5 %all-gather.14.cloned.1.call-done = bf16[4096,256]{1,0:T(8,128)(2,1)} async-done(((bf16[512,256]{1,0:T(8,128)(2,1)}), bf16[4096,256]{1,0:T(8,128)(2,1)}) %all-gather.14.cloned.1.call-update) | async-done | bytes 2097168 | tf_op jit(solution)/shard_map/all_gather | solution.py:33
  42.6 15.6 %while.177 = (s32[]{:T(128)}, f32[4,256]{1,0:T(4,128)S(1)}, f32[4,256]{1,0:T(4,128)S(1)}, f32[4096]{0:T(1024)}, f32[4,256]{1,0:T(4,128)S(1)}, /*index=5*/f32[409...) while((s32[]{:T(128)}, f32[4,256]{1,0:T(4,128)S(1)}, ...), condition=%wide.region_5.6_spmd, body=%wide.region_2.5_spmd.sunk | while | flops 547356160 | bytes 10660465 | solution.py:55
  58.3 13.3 %all-gather.6 = f32[4,1,1024]{2,1,0:T(1,128)S(1)} all-gather(f32[1,1,1024]{2,1,0:T(1,128)S(1)} %reshape.89), channel_id=1, replica_groups=mesh['row'=8,'col'=4] {'col'}, dimensions={0}, use_global_device_ids=true | all-gather | bytes 20480 | tf_op jit(solution)/shard_map/all_gather | solution.py:11
  71.5 13.2 %all-gather.7 = f32[4,1,1024]{2,1,0:T(1,128)S(1)} all-gather(f32[1,1,1024]{2,1,0:T(1,128)S(1)} %reshape.91), channel_id=1, replica_groups=mesh['row'=8,'col'=4] {'col'}, dimensions={0}, use_global_device_ids=true | all-gather | bytes 20480 | tf_op jit(solution)/shard_map/all_gather | solution.py:11
  85.0 15.2 %while.186 = (s32[]{:T(128)}, f32[4096]{0:T(1024)S(1)}, f32[4096]{0:T(1024)S(1)}, f32[4,256]{1,0:T(4,128)S(1)}, f32[4,256]{1,0:T(4,128)S(1)}, /*index=5*/f32[4,2...) while((s32[]{:T(128)}, f32[4096]{0:T(1024)S(1)}, ...), condition=%wide.region_11.12_spmd.clone, body=%wide.region_8.11_spmd.clone.sunk | while | flops 547381248 | bytes 10790527 | solution.py:75
  85.0 3.1 fusion.87
  96.4 3.1 fusion.87
  100.2 9.2 %all-gather = f32[32768]{0:T(1024)S(1)} all-gather(f32[4096]{0:T(1024)S(1)} %get-tuple-element.1088), channel_id=2, replica_groups=mesh['row'=8,'col'=4] {'row'}, dimensions={0}, use_global_device_ids=true | all-gather | bytes 147456 | tf_op jit(solution)/shard_map/all_gather | solution.py:11
  109.4 8.3 %all-gather.1 = f32[32768]{0:T(1024)S(1)} all-gather(f32[4096]{0:T(1024)S(1)} %get-tuple-element.1089), channel_id=3, replica_groups=mesh['row'=8,'col'=4] {'row'}, dimensions={0}, use_global_device_ids=true | all-gather | bytes 147456 | tf_op jit(solution)/shard_map/all_gather | solution.py:11
  118.3 16.0 %while.180 = (s32[]{:T(128)}, f32[4,256]{1,0:T(4,128)S(1)}, f32[4,256]{1,0:T(4,128)S(1)}, f32[4096]{0:T(1024)S(1)}, f32[4096]{0:T(1024)S(1)}, /*index=5*/f32[4,2...) while((s32[]{:T(128)}, f32[4,256]{1,0:T(4,128)S(1)}, ...), condition=%wide.region_17.18_spmd, body=%wide.region_14.17_spmd.sunk | while | flops 547356160 | bytes 10676857 | solution.py:55
  118.4 3.2 fusion.83
  122.4 3.2 fusion.83
  126.4 3.2 fusion.83
  130.4 3.2 fusion.83
  134.4 13.2 %all-gather.8 = f32[4,1,1024]{2,1,0:T(1,128)S(1)} all-gather(f32[1,1,1024]{2,1,0:T(1,128)S(1)} %reshape.93), channel_id=1, replica_groups=mesh['row'=8,'col'=4] {'col'}, dimensions={0}, use_global_device_ids=true | all-gather | bytes 20480 | tf_op jit(solution)/shard_map/all_gather | solution.py:11
  147.6 13.2 %all-gather.9 = f32[4,1,1024]{2,1,0:T(1,128)S(1)} all-gather(f32[1,1,1024]{2,1,0:T(1,128)S(1)} %reshape.95), channel_id=1, replica_groups=mesh['row'=8,'col'=4] {'col'}, dimensions={0}, use_global_device_ids=true | all-gather | bytes 20480 | tf_op jit(solution)/shard_map/all_gather | solution.py:11
  161.0 15.2 %while.187 = (s32[]{:T(128)}, f32[4096]{0:T(1024)S(1)}, f32[4096]{0:T(1024)S(1)}, f32[4,256]{1,0:T(4,128)S(1)}, f32[4,256]{1,0:T(4,128)S(1)}, /*index=5*/f32[4,2...) while((s32[]{:T(128)}, f32[4096]{0:T(1024)S(1)}, ...), condition=%wide.region_23.24_spmd.clone, body=%wide.region_20.23_spmd.clone.sunk | while | flops 547381248 | bytes 10790527 | solution.py:75
  161.1 3.1 fusion.90
  176.2 9.3 %all-gather.2 = f32[32768]{0:T(1024)S(1)} all-gather(f32[4096]{0:T(1024)S(1)} %get-tuple-element.1096), channel_id=4, replica_groups=mesh['row'=8,'col'=4] {'row'}, dimensions={0}, use_global_device_ids=true | all-gather | bytes 147456 | tf_op jit(solution)/shard_map/all_gather | solution.py:11
  185.6 8.3 %all-gather.3 = f32[32768]{0:T(1024)S(1)} all-gather(f32[4096]{0:T(1024)S(1)} %get-tuple-element.1097), channel_id=5, replica_groups=mesh['row'=8,'col'=4] {'row'}, dimensions={0}, use_global_device_ids=true | all-gather | bytes 147456 | tf_op jit(solution)/shard_map/all_gather | solution.py:11
  194.5 16.0 %while.183 = (s32[]{:T(128)}, f32[4,256]{1,0:T(4,128)S(1)}, f32[4,256]{1,0:T(4,128)S(1)}, f32[4096]{0:T(1024)S(1)}, f32[4096]{0:T(1024)S(1)}, /*index=5*/f32[4,2...) while((s32[]{:T(128)}, f32[4,256]{1,0:T(4,128)S(1)}, ...), condition=%wide.region_29.30_spmd, body=%wide.region_26.29_spmd.sunk | while | flops 547356160 | bytes 10676857 | solution.py:55
  194.6 3.2 fusion.85
  198.6 3.2 fusion.85
  202.6 3.2 fusion.85
  206.6 3.2 fusion.85
  210.6 13.2 %all-gather.10 = f32[4,1,1024]{2,1,0:T(1,128)S(1)} all-gather(f32[1,1,1024]{2,1,0:T(1,128)S(1)} %reshape.97), channel_id=1, replica_groups=mesh['row'=8,'col'=4] {'col'}, dimensions={0}, use_global_device_ids=true | all-gather | bytes 20480 | tf_op jit(solution)/shard_map/all_gather | solution.py:11
  223.8 13.2 %all-gather.11 = f32[4,1,1024]{2,1,0:T(1,128)S(1)} all-gather(f32[1,1,1024]{2,1,0:T(1,128)S(1)} %reshape.99), channel_id=1, replica_groups=mesh['row'=8,'col'=4] {'col'}, dimensions={0}, use_global_device_ids=true | all-gather | bytes 20480 | tf_op jit(solution)/shard_map/all_gather | solution.py:11
  238.4 15.2 %while.188 = (s32[]{:T(128)}, f32[4096]{0:T(1024)S(1)}, f32[4096]{0:T(1024)S(1)}, f32[4,256]{1,0:T(4,128)S(1)}, f32[4,256]{1,0:T(4,128)S(1)}, /*index=5*/f32[4,2...) while((s32[]{:T(128)}, f32[4096]{0:T(1024)S(1)}, ...), condition=%wide.region_35.36_spmd.clone, body=%wide.region_32.35_spmd.clone.sunk | while | flops 547381248 | bytes 10790527 | solution.py:75
  246.0 3.1 fusion.93
  253.6 9.2 %all-gather.4 = f32[32768]{0:T(1024)S(1)} all-gather(f32[4096]{0:T(1024)S(1)} %get-tuple-element.1104), channel_id=6, replica_groups=mesh['row'=8,'col'=4] {'row'}, dimensions={0}, use_global_device_ids=true | all-gather | bytes 147456 | tf_op jit(solution)/shard_map/all_gather | solution.py:11
  262.8 8.3 %all-gather.5 = f32[32768]{0:T(1024)S(1)} all-gather(f32[4096]{0:T(1024)S(1)} %get-tuple-element.1105), channel_id=7, replica_groups=mesh['row'=8,'col'=4] {'row'}, dimensions={0}, use_global_device_ids=true | all-gather | bytes 147456 | tf_op jit(solution)/shard_map/all_gather | solution.py:11
  274.3 39.1 %psum.7 = f32[]{:T(128)} all-reduce(f32[]{:T(128)S(6)} %add.464), channel_id=1, replica_groups=mesh['row'=8,'col'=4] {'row','col'}, use_global_device_ids=true, to_apply=%region_40.41 | all-reduce | flops 1 | bytes 8 | tf_op jit(solution)/shard_map/psum | solution.py:83
  (235 shorter events, 65.7 us)
Async XLA Ops:
  7.2 33.2 %all-gather.14.cloned.1.call-start = ((), (), s32[]{:S(2)}) async-start(), calls=%async_computation | async-start | bytes 2359296 | tf_op jit(solution)/shard_map/all_gather | solution.py:33
  85.0 33.3 %copy-start.1 = (f32[4096]{0:T(1024)S(1)}, f32[4096]{0:T(1024)}, u32[]{:S(2)}) copy-start(f32[4096]{0:T(1024)} %get-tuple-element.2387) | copy-start | bytes 49156
  237.8 0.6 copy-start
Sparse Core Ops, SparseCore 0:
  9.9 30.4 all-gather.13
where the time goes:
time: 322 us; the launch traced here: 320 us
  blocking collectives  171 us (53%)
  matrix products  75.1 us (23%)
  waiting for transfers between devices  31.2 us (10%)
  other arithmetic  22 us (7%)
  between operations  15.7 us (5%)
  local copies, waits for them, and re-layouts  3.61 us (1%)
    all_gather x12, blocking collectives, combined_all(): everything = jax.tree.map(lambda part: lax.all_gather(part, axis), value)  132 us
    dot_general x24, matrix products, cost_block(): lax.dot_general(points_a, points_b, (((1,), (1,)), ((), ())), preferred_e...  75.1 us
    psum x1, blocking collectives, body(): mean_potentials = lax.psum(local, ('row', 'col'))  39.1 us
    all_gather x1, waiting for transfers between devices, body(): targets = lax.all_gather(tgt_points, 'row', axis=0, tiled=True)  30.5 us
    reduce_sum x12, other arithmetic, row_pair(): return (top, jnp.sum(jnp.exp(terms - top[:, None]), axis=1))  8.61 us
    reduce_sum x12, other arithmetic, pair_step(): block_sum = jnp.sum(jnp.exp(terms - block_top[None, :]), axis=0)  7.15 us
  transfers between devices with their start and end apart: 1, of which 1 were waited for; matrix products, arithmetic and copies ran while one was open for 1% of the time, Pallas kernels for 0%

commit v1 on v0

--- a/solution.py
+++ b/solution.py
@@ -30,7 +30,21 @@
 
 
 def body(src_points, tgt_points, log_src_mass, log_tgt_mass):
-    targets = lax.all_gather(tgt_points, "row", axis=0, tiled=True)
+
+    def heads_test(load):
+        peer_axis = "row"
+        vals = [load]
+        n_blocks = lax.psum(1, peer_axis)
+        for rr in range(n_blocks - 1):
+            vals.append(
+                lax.ppermute(
+                    vals[-1], peer_axis, [(j0, (j0 + 1) % n_blocks) for j0 in range(n_blocks)]
+                )
+            )
+        low = jnp.concatenate(vals[::-1], axis=0)
+        return jnp.roll(low, (lax.axis_index(peer_axis) + 1) * load.shape[0], axis=0)
+
+    targets = heads_test(tgt_points)
     sqy = jnp.sum(targets.astype(jnp.float32) ** 2, axis=1)
     count = src_points.shape[0]
     block = min(256, count)

time: 322 us -> 282 us (0.88)
  matrix products: 75.1 us -> 35.4 us
  waiting for transfers between devices: 31.2 us -> 45.3 us
  between operations: 15.7 us -> 2.5 us
    ppermute x0 -> x7, waiting for transfers between devices: none -> 45.3 us  [heads_test(): lax.ppermute(vals[-1], peer_axis, [(j0, (j0 + 1) % n_blocks) for j0 in ra...]
    dot_general x24, matrix products: 75.1 us -> 35.4 us  [cost_block(): lax.dot_general(points_a, points_b, (((1,), (1,)), ((), ())), preferred_e...]
    all_gather x1 -> x0, waiting for transfers between devices: 30.5 us -> none  [body(): targets = lax.all_gather(tgt_points, 'row', axis=0, tiled=True)]
  transfers between devices with their start and end apart: 1 -> 7, of which waited for: 1 -> 7; matrix products, arithmetic and copies ran while one was open for 1% -> 1% of each run, Pallas kernels for 0% -> 0%
where the time goes in v1:
time: 282 us
  blocking collectives  172 us (61%)
  waiting for transfers between devices  45.3 us (16%)
  matrix products  35.4 us (13%)
  other arithmetic  20.4 us (7%)
  local copies, waits for them, and re-layouts  4.07 us (1%)
    all_gather x12, blocking collectives, combined_all(): everything = jax.tree.map(lambda part: lax.all_gather(part, axis), value)  133 us
    ppermute x7, waiting for transfers between devices, heads_test(): lax.ppermute(vals[-1], peer_axis, [(j0, (j0 + 1) % n_blocks) for j0 in ra...  45.3 us
    psum x1, blocking collectives, body(): mean_potentials = lax.psum(local, ('row', 'col'))  39.3 us
    dot_general x24, matrix products, cost_block(): lax.dot_general(points_a, points_b, (((1,), (1,)), ((), ())), preferred_e...  35.4 us
    reduce_sum x12, other arithmetic, row_pair(): return (top, jnp.sum(jnp.exp(terms - top[:, None]), axis=1))  8.61 us
    reduce_sum x12, other arithmetic, pair_step(): block_sum = jnp.sum(jnp.exp(terms - block_top[None, :]), axis=0)  7.15 us
  transfers between devices with their start and end apart: 7, of which 7 were waited for; matrix products, arithmetic and copies ran while one was open for 1% of the time, Pallas kernels for 0%

profile of v1, /device:TPU:0, one launch (start us, length us, event | category | flops | bytes accessed | tf_op | source)
XLA Modules:
  0.0 282.0 jit_solution(7732518427664228320)
XLA Ops:
  1.2 7.1 %collective-permute-done = bf16[512,256]{1,0:T(8,128)(2,1)S(1)} collective-permute-done((bf16[512,256]{1,0:T(8,128)(2,1)}, bf16[512,256]{1,0:T(8,128)(2,1)S(1)}, u32[]{:S(2)}, u32[]{:S(2)}) %collective-permute-start) | collective-permute-done | bytes 262176 | tf_op jit(solution)/shard_map/ppermute | solution.py:40
  8.3 6.7 %collective-permute-done.1 = bf16[512,256]{1,0:T(8,128)(2,1)S(1)} collective-permute-done((bf16[512,256]{1,0:T(8,128)(2,1)S(1)}, bf16[512,256]{1,0:T(8,128)(2,1)S(1)}, u32[]{:S(2)}, u32[]{:S(2)}) %collective-permute-start.1) | collective-permute-done | bytes 262176 | tf_op jit(solution)/shard_map/ppermute | solution.py:40
  15.0 6.7 %collective-permute-done.2 = bf16[512,256]{1,0:T(8,128)(2,1)S(1)} collective-permute-done((bf16[512,256]{1,0:T(8,128)(2,1)S(1)}, bf16[512,256]{1,0:T(8,128)(2,1)S(1)}, u32[]{:S(2)}, u32[]{:S(2)}) %collective-permute-start.2) | collective-permute-done | bytes 262176 | tf_op jit(solution)/shard_map/ppermute | solution.py:40
  21.7 6.7 %collective-permute-done.3 = bf16[512,256]{1,0:T(8,128)(2,1)S(1)} collective-permute-done((bf16[512,256]{1,0:T(8,128)(2,1)S(1)}, bf16[512,256]{1,0:T(8,128)(2,1)S(1)}, u32[]{:S(2)}, u32[]{:S(2)}) %collective-permute-start.3) | collective-permute-done | bytes 262176 | tf_op jit(solution)/shard_map/ppermute | solution.py:40
  28.4 6.7 %collective-permute-done.4 = bf16[512,256]{1,0:T(8,128)(2,1)S(1)} collective-permute-done((bf16[512,256]{1,0:T(8,128)(2,1)S(1)}, bf16[512,256]{1,0:T(8,128)(2,1)S(1)}, u32[]{:S(2)}, u32[]{:S(2)}) %collective-permute-start.4) | collective-permute-done | bytes 262176 | tf_op jit(solution)/shard_map/ppermute | solution.py:40
  35.1 6.7 %collective-permute-done.5 = bf16[512,256]{1,0:T(8,128)(2,1)S(1)} collective-permute-done((bf16[512,256]{1,0:T(8,128)(2,1)S(1)}, bf16[512,256]{1,0:T(8,128)(2,1)S(1)}, u32[]{:S(2)}, u32[]{:S(2)}) %collective-permute-start.5) | collective-permute-done | bytes 262176 | tf_op jit(solution)/shard_map/ppermute | solution.py:40
  43.8 4.7 %collective-permute-done.6 = bf16[512,256]{1,0:T(8,128)(2,1)S(1)} collective-permute-done((bf16[512,256]{1,0:T(8,128)(2,1)S(1)}, bf16[512,256]{1,0:T(8,128)(2,1)S(1)}, u32[]{:S(2)}, u32[]{:S(2)}) %collective-permute-start.6) | collective-permute-done | bytes 262176 | tf_op jit(solution)/shard_map/ppermute | solution.py:40
  49.8 9.3 %while.177 = (s32[]{:T(128)}, f32[4,256]{1,0:T(4,128)S(1)}, f32[4,256]{1,0:T(4,128)S(1)}, f32[4096]{0:T(1024)S(1)}, f32[4,256]{1,0:T(4,128)S(1)}, /*index=5*/f32...) while((s32[]{:T(128)}, f32[4,256]{1,0:T(4,128)S(1)}, ...), condition=%wide.region_5.6_spmd, body=%wide.region_2.5_spmd.sunk | while | flops 547356160 | bytes 10659957 | solution.py:69
  59.1 14.2 %all-gather.6 = f32[4,1,1024]{2,1,0:T(1,128)S(1)} all-gather(f32[1,1,1024]{2,1,0:T(1,128)S(1)} %reshape.89), channel_id=1, replica_groups=mesh['row'=8,'col'=4] {'col'}, dimensions={0}, use_global_device_ids=true | all-gather | bytes 20480 | tf_op jit(solution)/shard_map/all_gather | solution.py:11
  73.3 13.2 %all-gather.7 = f32[4,1,1024]{2,1,0:T(1,128)S(1)} all-gather(f32[1,1,1024]{2,1,0:T(1,128)S(1)} %reshape.91), channel_id=1, replica_groups=mesh['row'=8,'col'=4] {'col'}, dimensions={0}, use_global_device_ids=true | all-gather | bytes 20480 | tf_op jit(solution)/shard_map/all_gather | solution.py:11
  86.7 8.5 %while.186 = (s32[]{:T(128)}, f32[4096]{0:T(1024)S(1)}, f32[4096]{0:T(1024)S(1)}, f32[4,256]{1,0:T(4,128)S(1)}, f32[4,256]{1,0:T(4,128)S(1)}, /*index=5*/f32[4,2...) while((s32[]{:T(128)}, f32[4096]{0:T(1024)S(1)}, ...), condition=%wide.region_11.12_spmd.clone, body=%wide.region_8.11_spmd.clone.sunk | while | flops 547381248 | bytes 10790019 | solution.py:89
  95.2 9.2 %all-gather = f32[32768]{0:T(1024)S(1)} all-gather(f32[4096]{0:T(1024)S(1)} %get-tuple-element.1088), channel_id=2, replica_groups=mesh['row'=8,'col'=4] {'row'}, dimensions={0}, use_global_device_ids=true | all-gather | bytes 147456 | tf_op jit(solution)/shard_map/all_gather | solution.py:11
  104.5 8.2 %all-gather.1 = f32[32768]{0:T(1024)S(1)} all-gather(f32[4096]{0:T(1024)S(1)} %get-tuple-element.1089), channel_id=3, replica_groups=mesh['row'=8,'col'=4] {'row'}, dimensions={0}, use_global_device_ids=true | all-gather | bytes 147456 | tf_op jit(solution)/shard_map/all_gather | solution.py:11
  113.3 9.4 %while.180 = (s32[]{:T(128)}, f32[4,256]{1,0:T(4,128)S(1)}, f32[4,256]{1,0:T(4,128)S(1)}, f32[4096]{0:T(1024)S(1)}, f32[4096]{0:T(1024)S(1)}, /*index=5*/f32[4,2...) while((s32[]{:T(128)}, f32[4,256]{1,0:T(4,128)S(1)}, ...), condition=%wide.region_17.18_spmd, body=%wide.region_14.17_spmd.sunk | while | flops 547356160 | bytes 10676349 | solution.py:69
  115.7 1.5 fusion.83
  118.0 1.5 fusion.83
  120.4 1.5 fusion.83
  122.7 13.2 %all-gather.8 = f32[4,1,1024]{2,1,0:T(1,128)S(1)} all-gather(f32[1,1,1024]{2,1,0:T(1,128)S(1)} %reshape.93), channel_id=1, replica_groups=mesh['row'=8,'col'=4] {'col'}, dimensions={0}, use_global_device_ids=true | all-gather | bytes 20480 | tf_op jit(solution)/shard_map/all_gather | solution.py:11
  136.0 13.4 %all-gather.9 = f32[4,1,1024]{2,1,0:T(1,128)S(1)} all-gather(f32[1,1,1024]{2,1,0:T(1,128)S(1)} %reshape.95), channel_id=1, replica_groups=mesh['row'=8,'col'=4] {'col'}, dimensions={0}, use_global_device_ids=true | all-gather | bytes 20480 | tf_op jit(solution)/shard_map/all_gather | solution.py:11
  149.6 8.5 %while.187 = (s32[]{:T(128)}, f32[4096]{0:T(1024)S(1)}, f32[4096]{0:T(1024)S(1)}, f32[4,256]{1,0:T(4,128)S(1)}, f32[4,256]{1,0:T(4,128)S(1)}, /*index=5*/f32[4,2...) while((s32[]{:T(128)}, f32[4096]{0:T(1024)S(1)}, ...), condition=%wide.region_23.24_spmd.clone, body=%wide.region_20.23_spmd.clone.sunk | while | flops 547381248 | bytes 10790019 | solution.py:89
  158.0 9.2 %all-gather.2 = f32[32768]{0:T(1024)S(1)} all-gather(f32[4096]{0:T(1024)S(1)} %get-tuple-element.1096), channel_id=4, replica_groups=mesh['row'=8,'col'=4] {'row'}, dimensions={0}, use_global_device_ids=true | all-gather | bytes 147456 | tf_op jit(solution)/shard_map/all_gather | solution.py:11
  167.3 8.2 %all-gather.3 = f32[32768]{0:T(1024)S(1)} all-gather(f32[4096]{0:T(1024)S(1)} %get-tuple-element.1097), channel_id=5, replica_groups=mesh['row'=8,'col'=4] {'row'}, dimensions={0}, use_global_device_ids=true | all-gather | bytes 147456 | tf_op jit(solution)/shard_map/all_gather | solution.py:11
  176.2 9.4 %while.183 = (s32[]{:T(128)}, f32[4,256]{1,0:T(4,128)S(1)}, f32[4,256]{1,0:T(4,128)S(1)}, f32[4096]{0:T(1024)S(1)}, f32[4096]{0:T(1024)S(1)}, /*index=5*/f32[4,2...) while((s32[]{:T(128)}, f32[4,256]{1,0:T(4,128)S(1)}, ...), condition=%wide.region_29.30_spmd, body=%wide.region_26.29_spmd.sunk | while | flops 547356160 | bytes 10676349 | solution.py:69
  178.5 1.5 fusion.85
  180.9 1.5 fusion.85
  183.2 1.5 fusion.85
  185.6 13.2 %all-gather.10 = f32[4,1,1024]{2,1,0:T(1,128)S(1)} all-gather(f32[1,1,1024]{2,1,0:T(1,128)S(1)} %reshape.97), channel_id=1, replica_groups=mesh['row'=8,'col'=4] {'col'}, dimensions={0}, use_global_device_ids=true | all-gather | bytes 20480 | tf_op jit(solution)/shard_map/all_gather | solution.py:11
  198.8 13.2 %all-gather.11 = f32[4,1,1024]{2,1,0:T(1,128)S(1)} all-gather(f32[1,1,1024]{2,1,0:T(1,128)S(1)} %reshape.99), channel_id=1, replica_groups=mesh['row'=8,'col'=4] {'col'}, dimensions={0}, use_global_device_ids=true | all-gather | bytes 20480 | tf_op jit(solution)/shard_map/all_gather | solution.py:11
  213.4 8.4 %while.188 = (s32[]{:T(128)}, f32[4096]{0:T(1024)S(1)}, f32[4096]{0:T(1024)S(1)}, f32[4,256]{1,0:T(4,128)S(1)}, f32[4,256]{1,0:T(4,128)S(1)}, /*index=5*/f32[4,2...) while((s32[]{:T(128)}, f32[4096]{0:T(1024)S(1)}, ...), condition=%wide.region_35.36_spmd.clone, body=%wide.region_32.35_spmd.clone.sunk | while | flops 547381248 | bytes 10790019 | solution.py:89
  221.9 9.2 %all-gather.4 = f32[32768]{0:T(1024)S(1)} all-gather(f32[4096]{0:T(1024)S(1)} %get-tuple-element.1104), channel_id=6, replica_groups=mesh['row'=8,'col'=4] {'row'}, dimensions={0}, use_global_device_ids=true | all-gather | bytes 147456 | tf_op jit(solution)/shard_map/all_gather | solution.py:11
  231.2 8.2 %all-gather.5 = f32[32768]{0:T(1024)S(1)} all-gather(f32[4096]{0:T(1024)S(1)} %get-tuple-element.1105), channel_id=7, replica_groups=mesh['row'=8,'col'=4] {'row'}, dimensions={0}, use_global_device_ids=true | all-gather | bytes 147456 | tf_op jit(solution)/shard_map/all_gather | solution.py:11
  242.6 39.3 %psum.7 = f32[]{:T(128)} all-reduce(f32[]{:T(128)S(6)} %add.480), channel_id=1, replica_groups=mesh['row'=8,'col'=4] {'row','col'}, use_global_device_ids=true, to_apply=%region_40.41 | all-reduce | flops 1 | bytes 8 | tf_op jit(solution)/shard_map/psum | solution.py:97
  (266 shorter events, 53.5 us)
Async XLA Ops:
  0.6 48.1 %copy-start = (bf16[512,256]{1,0:T(8,128)(2,1)S(1)}, bf16[512,256]{1,0:T(8,128)(2,1)}, u32[]{:S(2)}) copy-start(bf16[512,256]{1,0:T(8,128)(2,1)} %param.29) | copy-start | bytes 786436
  0.6 7.7 %collective-permute-start = (bf16[512,256]{1,0:T(8,128)(2,1)}, bf16[512,256]{1,0:T(8,128)(2,1)S(1)}, u32[]{:S(2)}, u32[]{:S(2)}) collective-permute-start(bf16[512,256]{1,0:T(8,128)(2,1)} %param.29), channel_id=1, source_target_pairs={{0,4},{4,8},{8,12},{12,16},{16,20},{20,24},{24,28},{28,0},{1,5},{5... | collective-permute-start | bytes 786440 | tf_op jit(solution)/shard_map/ppermute | solution.py:40
  8.3 6.7 %collective-permute-start.1 = (bf16[512,256]{1,0:T(8,128)(2,1)S(1)}, bf16[512,256]{1,0:T(8,128)(2,1)S(1)}, u32[]{:S(2)}, u32[]{:S(2)}) collective-permute-start(bf16[512,256]{1,0:T(8,128)(2,1)S(1)} %collective-permute-done), channel_id=1, source_target_pairs={{0,4},{4,8},{8,12},{12,16},{16,20},{20,24},{24,28},{28,0},{1,5},{5... | collective-permute-start | bytes 786440 | tf_op jit(solution)/shard_map/ppermute | solution.py:40
  15.0 6.7 %collective-permute-start.2 = (bf16[512,256]{1,0:T(8,128)(2,1)S(1)}, bf16[512,256]{1,0:T(8,128)(2,1)S(1)}, u32[]{:S(2)}, u32[]{:S(2)}) collective-permute-start(bf16[512,256]{1,0:T(8,128)(2,1)S(1)} %collective-permute-done.1), channel_id=1, source_target_pairs={{0,4},{4,8},{8,12},{12,16},{16,20},{20,24},{24,28},{28,0},{1,5},{5... | collective-permute-start | bytes 786440 | tf_op jit(solution)/shard_map/ppermute | solution.py:40
  21.7 6.7 %collective-permute-start.3 = (bf16[512,256]{1,0:T(8,128)(2,1)S(1)}, bf16[512,256]{1,0:T(8,128)(2,1)S(1)}, u32[]{:S(2)}, u32[]{:S(2)}) collective-permute-start(bf16[512,256]{1,0:T(8,128)(2,1)S(1)} %collective-permute-done.2), channel_id=1, source_target_pairs={{0,4},{4,8},{8,12},{12,16},{16,20},{20,24},{24,28},{28,0},{1,5},{5... | collective-permute-start | bytes 786440 | tf_op jit(solution)/shard_map/ppermute | solution.py:40
  28.4 6.7 %collective-permute-start.4 = (bf16[512,256]{1,0:T(8,128)(2,1)S(1)}, bf16[512,256]{1,0:T(8,128)(2,1)S(1)}, u32[]{:S(2)}, u32[]{:S(2)}) collective-permute-start(bf16[512,256]{1,0:T(8,128)(2,1)S(1)} %collective-permute-done.3), channel_id=1, source_target_pairs={{0,4},{4,8},{8,12},{12,16},{16,20},{20,24},{24,28},{28,0},{1,5},{5... | collective-permute-start | bytes 786440 | tf_op jit(solution)/shard_map/ppermute | solution.py:40
  35.1 6.7 %collective-permute-start.5 = (bf16[512,256]{1,0:T(8,128)(2,1)S(1)}, bf16[512,256]{1,0:T(8,128)(2,1)S(1)}, u32[]{:S(2)}, u32[]{:S(2)}) collective-permute-start(bf16[512,256]{1,0:T(8,128)(2,1)S(1)} %collective-permute-done.4), channel_id=1, source_target_pairs={{0,4},{4,8},{8,12},{12,16},{16,20},{20,24},{24,28},{28,0},{1,5},{5... | collective-permute-start | bytes 786440 | tf_op jit(solution)/shard_map/ppermute | solution.py:40
  41.8 6.7 %collective-permute-start.6 = (bf16[512,256]{1,0:T(8,128)(2,1)S(1)}, bf16[512,256]{1,0:T(8,128)(2,1)S(1)}, u32[]{:S(2)}, u32[]{:S(2)}) collective-permute-start(bf16[512,256]{1,0:T(8,128)(2,1)S(1)} %collective-permute-done.5), channel_id=1, source_target_pairs={{0,4},{4,8},{8,12},{12,16},{16,20},{20,24},{24,28},{28,0},{1,5},{5... | collective-permute-start | bytes 786440 | tf_op jit(solution)/shard_map/ppermute | solution.py:40
  48.7 1.0 copy-start.1
  48.7 1.0 copy-start.3
  212.8 0.6 copy-start.2
